TPU v7x, 32 devices: a whole 2x2x4 slice. The times are simulated.
32 devices in a mesh: dp: 4 (over y, x), seq: 8 (over z, core).
Axes of the slice: x: 2, y: 2, z: 4, core: 2. Of those that a mesh axis runs over, the one named last changes fastest.
Arguments:
- hidden_in: bfloat16 [4, 2048, 1536], P('dp', 'seq'), may hold values from -6 to 6
- pre_gain: bfloat16 [1536], P('dp'), may hold values from 0.5 to 1.5
- in_weight: bfloat16 [1536, 6448], P('dp'), may hold values from -0.15625 to 0.15625
- conv_x_weight: float32 [4, 3072], replicated, may hold values from -3 to 3
- conv_x_bias: float32 [3072], replicated, may hold values from -3 to 3
- conv_bc_weight: float32 [4, 256], replicated, may hold values from -3 to 3
- conv_bc_bias: float32 [256], replicated, may hold values from -3 to 3
- dt_bias: float32 [48], replicated, may hold values from -5 to -2
- a_log: float32 [48], replicated, may hold values from -4.5 to 2.8
- skip: float32 [48], replicated, may hold values from 0.5 to 1.5
- norm_gain: bfloat16 [3072], P('dp'), may hold values from 0.5 to 1.5
- out_weight: bfloat16 [3072, 1536], P('dp'), may hold values from -0.109375 to 0.109375
- output_gradient: bfloat16 [4, 2048, 1536], P('dp', 'seq'), may hold values from -6 to 6
Outputs:
- output: float32 [4, 2048, 1536], P('dp', 'seq')
- input_grad: float32 [4, 2048, 1536], P('dp', 'seq')
- pre_gain_grad: float32 [1536], P('dp')
- in_weight_grad: float32 [1536, 6448], P('dp')
- conv_x_weight_grad: float32 [4, 3072], replicated
- conv_x_bias_grad: float32 [3072], replicated
- conv_bc_weight_grad: float32 [4, 256], replicated
- conv_bc_bias_grad: float32 [256], replicated
- dt_bias_grad: float32 [48], replicated
- a_log_grad: float32 [48], replicated
- skip_grad: float32 [48], replicated
- norm_gain_grad: float32 [3072], P('dp')
- out_weight_grad: float32 [3072, 1536], P('dp')
All inputs are finite; a program needn't handle non-finite values.
Results may differ from a plain program's by a relative error of at most 0.008.
The roundings to bfloat16 on the way count: a program that leaves them out, or rounds other values in their place, can miss the bound.
Values may be sent and summed in bfloat16 or wider, within the bound.
A program may use at most 256 MiB of HBM per device.

v0:
```python
import jax
import jax.numpy as jnp
from jax import lax
from jax.sharding import PartitionSpec as P

BLOCK = 256


EPSILON = 1e-05
PRECISE = lax.Precision.HIGHEST


def causal_conv(signal, kernel, offset):
    tap_count = kernel.shape[0]
    length = signal.shape[0]
    padded = jnp.pad(signal, ((tap_count - 1, 0), (0, 0)))
    summed_taps = jnp.zeros_like(signal) + offset[None, :]
    for tap_index in range(tap_count):
        summed_taps = (
            summed_taps + kernel[tap_index][None, :] * padded[tap_index : tap_index + length]
        )
    return summed_taps


def block_scan(values, step_sizes, decay_rates, key_rows, queries):
    length, head_count, head_width = values.shape
    block_count = length // BLOCK
    log_decay = (step_sizes * decay_rates[None, :]).reshape(block_count, BLOCK, head_count)
    lower_mask = lax.broadcasted_iota(jnp.int32, (BLOCK, BLOCK), 0) >= lax.broadcasted_iota(
        jnp.int32, (BLOCK, BLOCK), 1
    )
    cumulative = jnp.einsum(
        "ij,cjh->cih", lower_mask.astype(jnp.float32), log_decay, precision=PRECISE
    )
    value_blocks = values.reshape(block_count, BLOCK, head_count, head_width)
    step_blocks = step_sizes.reshape(block_count, BLOCK, head_count)
    key_blocks = key_rows.reshape(block_count, BLOCK, -1)
    query_blocks = queries.reshape(block_count, BLOCK, -1)
    scores = jnp.einsum("cin,cjn->cij", query_blocks, key_blocks, precision=PRECISE)
    spread = cumulative[:, :, None, :] - cumulative[:, None, :, :]
    decay_table = jnp.exp(jnp.where(lower_mask[None, :, :, None], spread, -1e30))
    mixing = scores[:, :, :, None] * decay_table * step_blocks[:, None, :, :]
    inside = jnp.einsum("cijh,cjhp->cihp", mixing, value_blocks, precision=PRECISE)
    tail_decay = jnp.exp(cumulative[:, -1:, :] - cumulative) * step_blocks
    fresh_state = jnp.einsum(
        "cjn,cjh,cjhp->chnp", key_blocks, tail_decay, value_blocks, precision=PRECISE
    )
    block_log = cumulative[:, -1, :]
    block_rows = lax.broadcasted_iota(jnp.int32, (block_count, block_count), 0)
    block_cols = lax.broadcasted_iota(jnp.int32, (block_count, block_count), 1)
    through = jnp.einsum(
        "de,eh->dh", (block_rows >= block_cols).astype(jnp.float32), block_log, precision=PRECISE
    )
    before = through - block_log
    block_spread = before[:, None, :] - through[None, :, :]
    block_weights = jnp.exp(jnp.where((block_rows > block_cols)[:, :, None], block_spread, -1e30))
    entering = jnp.einsum("deh,ehnp->dhnp", block_weights, fresh_state, precision=PRECISE)
    outside = jnp.einsum(
        "cin,cih,chnp->cihp", query_blocks, jnp.exp(cumulative), entering, precision=PRECISE
    )
    return (inside + outside).reshape(length, head_count, head_width)


def mixer(
    x_raw, dt_raw, bc_raw, conv_weight, conv_bias, bc_weight, bc_bias, dt_shift, a_logs, skip_gain
):
    head_count = dt_raw.shape[1]
    length = x_raw.shape[0]
    state_width = bc_raw.shape[1] // 2
    values = jax.nn.silu(causal_conv(x_raw, conv_weight, conv_bias)).reshape(length, head_count, -1)
    key_query = jax.nn.silu(causal_conv(bc_raw, bc_weight, bc_bias))
    step_sizes = jax.nn.softplus(dt_raw + dt_shift[None, :])
    decay_rates = -jnp.exp(a_logs)
    scanned = block_scan(
        values, step_sizes, decay_rates, key_query[:, :state_width], key_query[:, state_width:]
    )
    scanned = scanned + skip_gain[None, :, None] * values
    return scanned.reshape(length, -1)


def batched_mixer(
    x_raw, dt_raw, bc_raw, conv_weight, conv_bias, bc_weight, bc_bias, dt_shift, a_logs, skip_gain
):
    mapped = jax.vmap(mixer, in_axes=(0, 0, 0, None, None, None, None, None, None, None))
    return mapped(
        x_raw,
        dt_raw,
        bc_raw,
        conv_weight,
        conv_bias,
        bc_weight,
        bc_bias,
        dt_shift,
        a_logs,
        skip_gain,
    )


def on_device(
    hidden_in,
    pre_gain,
    in_weight,
    conv_x_weight,
    conv_x_bias,
    conv_bc_weight,
    conv_bc_bias,
    dt_bias,
    a_log,
    skip,
    norm_gain,
    out_weight,
    output_gradient,
):
    seq_count = lax.axis_size("seq")
    data_count = lax.axis_size("dp")
    seq_rank = lax.axis_index("seq")
    inner_width = conv_x_bias.shape[0]
    state_width = conv_bc_bias.shape[0] // 2
    head_total = dt_bias.shape[0]
    head_dev = head_total // seq_count
    width_dev = inner_width // seq_count
    model_width = hidden_in.shape[2]
    complete_input, full_pre = (
        lax.all_gather(in_weight, "dp", axis=0, tiled=True),
        lax.all_gather(pre_gain, "dp", axis=0, tiled=True),
    )
    pre_float = full_pre.astype(jnp.float32)
    rows_float = hidden_in.astype(jnp.float32)
    inv_rms = lax.rsqrt(jnp.mean(rows_float * rows_float, -1, keepdims=True) + EPSILON)
    unit_rows = rows_float * inv_rms
    normalized_rows = (unit_rows * pre_float).astype(jnp.bfloat16)
    projected = lax.optimization_barrier(
        jnp.einsum(
            "vha,ay->vhy", normalized_rows, complete_input, preferred_element_type=jnp.float32
        ).astype(jnp.bfloat16)
    )
    proj_width = projected.shape[2]
    gate_float = projected[:, :, :inner_width].astype(jnp.float32)
    x_raw = projected[:, :, inner_width : 2 * inner_width]
    bc_raw = projected[:, :, 2 * inner_width : 2 * inner_width + 2 * state_width]
    dt_raw = projected[:, :, 2 * inner_width + 2 * state_width :]
    x_heads, dt_heads = (
        lax.all_to_all(x_raw, "seq", split_axis=2, concat_axis=1, tiled=True),
        lax.all_to_all(dt_raw, "seq", split_axis=2, concat_axis=1, tiled=True),
    )
    bc_whole = lax.all_gather(bc_raw, "seq", axis=1, tiled=True)
    conv_weight = lax.dynamic_slice_in_dim(conv_x_weight, seq_rank * width_dev, width_dev, 1)
    conv_bias = lax.dynamic_slice_in_dim(conv_x_bias, seq_rank * width_dev, width_dev, 0)
    dt_shift = lax.dynamic_slice_in_dim(dt_bias, seq_rank * head_dev, head_dev, 0)
    a_logs = lax.dynamic_slice_in_dim(a_log, seq_rank * head_dev, head_dev, 0)
    skip_gain = lax.dynamic_slice_in_dim(skip, seq_rank * head_dev, head_dev, 0)
    small_params = (
        conv_weight,
        conv_bias,
        conv_bc_weight,
        conv_bc_bias,
        dt_shift,
        a_logs,
        skip_gain,
    )
    mixer_out, pull_back = jax.vjp(
        batched_mixer,
        x_heads.astype(jnp.float32),
        dt_heads.astype(jnp.float32),
        bc_whole.astype(jnp.float32),
        *small_params
    )
    y_heads = mixer_out.astype(jnp.bfloat16)
    y_tokens = lax.all_to_all(y_heads, "seq", split_axis=1, concat_axis=2, tiled=True)
    complete_output, full_norm = (
        lax.all_gather(out_weight, "dp", axis=0, tiled=True),
        lax.all_gather(norm_gain, "dp", axis=0, tiled=True),
    )
    norm_float = full_norm.astype(jnp.float32)
    y_float = y_tokens.astype(jnp.float32)
    gate_sig = jax.nn.sigmoid(gate_float)
    gated_rows = y_float * gate_float * gate_sig
    out_rms = lax.rsqrt(jnp.mean(gated_rows * gated_rows, -1, keepdims=True) + EPSILON)
    unit_gated = gated_rows * out_rms
    mixer_result_rows = (unit_gated * norm_float).astype(jnp.bfloat16)
    output = rows_float + jnp.einsum(
        "ubc,cx->ubx", mixer_result_rows, complete_output, preferred_element_type=jnp.float32
    )
    out_weight_part = jnp.einsum(
        "bjo,bjf->of", mixer_result_rows, output_gradient, preferred_element_type=jnp.float32
    )
    mixer_rows_gradient = jnp.einsum(
        "wbg,jg->wbj", output_gradient, complete_output, preferred_element_type=jnp.float32
    )
    norm_gain_part = jnp.sum(mixer_rows_gradient * unit_gated, (0, 1))
    grad_unit = mixer_rows_gradient * norm_float
    grad_gated = out_rms * (
        grad_unit - unit_gated * jnp.mean(grad_unit * unit_gated, -1, keepdims=True)
    )
    grad_y = (grad_gated * gate_float * gate_sig).astype(jnp.bfloat16)
    grad_gate = grad_gated * y_float * gate_sig * (1.0 + gate_float * (1.0 - gate_sig))
    grad_y_heads = lax.all_to_all(grad_y, "seq", split_axis=2, concat_axis=1, tiled=True)
    pulled = pull_back(grad_y_heads.astype(jnp.float32))
    grad_x_tok, grad_dt_tok = (
        lax.all_to_all(
            pulled[0].astype(jnp.bfloat16), "seq", split_axis=1, concat_axis=2, tiled=True
        ),
        lax.all_to_all(
            pulled[1].astype(jnp.bfloat16), "seq", split_axis=1, concat_axis=2, tiled=True
        ),
    )
    grad_bc_tok = lax.psum_scatter(pulled[2], "seq", scatter_dimension=1, tiled=True)
    projection_gradient = jnp.concatenate(
        [grad_gate.astype(jnp.bfloat16), grad_x_tok, grad_bc_tok.astype(jnp.bfloat16), grad_dt_tok],
        -1,
    )
    in_weight_part = jnp.einsum(
        "hrx,hrw->xw", normalized_rows, projection_gradient, preferred_element_type=jnp.float32
    )
    normalized_gradient = jnp.einsum(
        "gnq,cq->gnc", projection_gradient, complete_input, preferred_element_type=jnp.float32
    )
    pre_gain_part = jnp.sum(normalized_gradient * unit_rows, (0, 1))
    grad_unit_rows = normalized_gradient * pre_float
    input_grad = output_gradient.astype(jnp.float32) + inv_rms * (
        grad_unit_rows - unit_rows * jnp.mean(grad_unit_rows * unit_rows, -1, keepdims=True)
    )
    local_small = pulled[3:]
    conv_weight_full = lax.dynamic_update_slice_in_dim(
        jnp.zeros(conv_x_weight.shape, jnp.float32), local_small[0], seq_rank * width_dev, 1
    )
    conv_bias_full = lax.dynamic_update_slice_in_dim(
        jnp.zeros(conv_x_bias.shape, jnp.float32), local_small[1], seq_rank * width_dev, 0
    )
    dt_full = lax.dynamic_update_slice_in_dim(
        jnp.zeros((head_total,), jnp.float32), local_small[4], seq_rank * head_dev, 0
    )
    alog_full = lax.dynamic_update_slice_in_dim(
        jnp.zeros((head_total,), jnp.float32), local_small[5], seq_rank * head_dev, 0
    )
    skip_full = lax.dynamic_update_slice_in_dim(
        jnp.zeros((head_total,), jnp.float32), local_small[6], seq_rank * head_dev, 0
    )
    summed_small = lax.psum(
        (
            conv_weight_full,
            conv_bias_full,
            local_small[2],
            local_small[3],
            dt_full,
            alog_full,
            skip_full,
        ),
        ("dp", "seq"),
    )
    device_total = data_count * seq_count
    grad_parts = (
        in_weight_part.reshape(device_total, -1, proj_width),
        pre_gain_part.reshape(device_total, -1),
        out_weight_part.reshape(device_total, -1, model_width),
        norm_gain_part.reshape(device_total, -1),
    )
    own_rows = (
        lax.psum_scatter(grad_parts[0], ("dp", "seq"), scatter_dimension=0, tiled=True),
        lax.psum_scatter(grad_parts[1], ("dp", "seq"), scatter_dimension=0, tiled=True),
        lax.psum_scatter(grad_parts[2], ("dp", "seq"), scatter_dimension=0, tiled=True),
        lax.psum_scatter(grad_parts[3], ("dp", "seq"), scatter_dimension=0, tiled=True),
    )
    whole_rows = (
        lax.all_gather(own_rows[0], "seq", axis=0, tiled=True),
        lax.all_gather(own_rows[1], "seq", axis=0, tiled=True),
        lax.all_gather(own_rows[2], "seq", axis=0, tiled=True),
        lax.all_gather(own_rows[3], "seq", axis=0, tiled=True),
    )
    in_weight_grad = whole_rows[0].reshape(-1, proj_width)
    pre_gain_grad = whole_rows[1].reshape(-1)
    out_weight_grad = whole_rows[2].reshape(-1, model_width)
    norm_gain_grad = whole_rows[3].reshape(-1)
    return (
        output,
        input_grad,
        pre_gain_grad,
        in_weight_grad,
        summed_small[0],
        summed_small[1],
        summed_small[2],
        summed_small[3],
        summed_small[4],
        summed_small[5],
        summed_small[6],
        norm_gain_grad,
        out_weight_grad,
    )


def solution(mesh):
    return jax.shard_map(
        on_device,
        mesh=mesh,
        in_specs=(
            P("dp", "seq", None),
            P("dp"),
            P("dp", None),
            P(),
            P(),
            P(),
            P(),
            P(),
            P(),
            P(),
            P("dp"),
            P("dp", None),
            P("dp", "seq", None),
        ),
        out_specs=(
            P("dp", "seq", None),
            P("dp", "seq", None),
            P("dp"),
            P("dp", None),
            P(),
            P(),
            P(),
            P(),
            P(),
            P(),
            P(),
            P("dp"),
            P("dp", None),
        ),
        check_vma=False,
    )
```

profile of v0, /device:TPU:0, one launch (start us, length us, event | category | flops | bytes accessed | tf_op | source)
XLA Modules:
  0.0 1579.8 jit_solution(6457453223499461496)
XLA Ops:
  8.0 9.6 all-gather
  17.9 178.1 %all-gather.10.cloned.1.call-done = bf16[1536,6448]{0,1:T(8,128)(2,1)} async-done(((bf16[384,6448]{0,1:T(8,128)(2,1)}), bf16[1536,6448]{0,1:T(8,128)(2,1)}) %all-gather.10.cloned.1.call-update) | async-done | bytes 19808272 | tf_op jit(solution)/shard_map/all_gather | solution.py:124
  196.0 10.0 fusion.3
  214.2 17.5 %copy.645 = bf16[1,256,3072]{1,0,2:T(2,128)(2,1)S(1)} copy(bf16[1,256,3072]{1,2,0:T(8,128)(2,1)S(1)} %slice.90) | data formatting | bytes 3145728 | tf_op jit(solution)/shard_map/slice | solution.py:139
  231.7 16.7 %reduce.51 = bf16[3072,256]{1,0:T(8,128)(2,1)} reduce(bf16[3072,1,256]{2,1,0:T(2,128)(2,1)S(1)} %bitcast.487, bf16[]{:T(256)} %broadcast.508), dimensions={1}, to_apply=%bitcast.470.reduce_sub_computation | reduce | bytes 3145730
  275.5 20.0 %all-to-all-done = bf16[8,2,49152]{2,1,0:T(2,128)(2,1)} async-done(((bf16[8,2,49152]{2,1,0:T(2,128)(2,1)}), bf16[8,2,49152]{2,1,0:T(2,128)(2,1)}, u32[]{:S(2)}, u32[]{:S(2)}) %all-to-all-start) | async-done | bytes 1572896 | tf_op jit(solution)/shard_map/all_to_all | solution.py:143
  327.3 15.2 bitcast_add_fusion.1
  358.1 28.4 %copy.644 = bf16[1,2048,384]{2,0,1:T(2,128)(2,1)} copy(bf16[1,2048,384]{2,1,0:T(8,128)(2,1)S(1)} %add_convert_fusion) | data formatting | bytes 3145728 | tf_op jit(solution)/shard_map/convert_element_type | solution.py:168
  386.5 35.5 %reduce.53 = bf16[2048,384]{1,0:T(8,128)(2,1)} reduce(bf16[2048,1,384]{2,1,0:T(2,128)(2,1)} %bitcast.490, bf16[]{:T(256)} %broadcast.508), dimensions={1}, to_apply=%bitcast.469.reduce_sub_computation | reduce | bytes 3145730
  430.1 8.1 all-gather.1
  438.2 29.6 %all-to-all-done.2 = bf16[8,2,49152]{2,1,0:T(2,128)(2,1)} async-done(((bf16[8,2,49152]{2,1,0:T(2,128)(2,1)}), bf16[8,2,49152]{2,1,0:T(2,128)(2,1)}, u32[]{:S(2)}, u32[]{:S(2)}) %all-to-all-start.2) | async-done | bytes 1572896 | tf_op jit(solution)/shard_map/all_to_all | solution.py:169
  487.4 8.8 fusion.40
  501.1 18.9 %copy.643 = bf16[1,256,3072]{1,0,2:T(2,128)(2,1)} copy(bf16[1,256,3072]{1,2,0:T(8,128)(2,1)S(1)} %get-tuple-element.149) | data formatting | bytes 3145728 | tf_op jit(solution)/shard_map/convert_element_type | solution.py:195
  520.1 17.8 %reduce.54 = bf16[3072,256]{1,0:T(8,128)(2,1)} reduce(bf16[3072,1,256]{2,1,0:T(2,128)(2,1)} %bitcast.492, bf16[]{:T(256)} %broadcast.508), dimensions={1}, to_apply=%bitcast.468.reduce_sub_computation | reduce | bytes 3145730
  541.5 42.6 %all_to_all.78 = bf16[8,2,49152]{2,1,0:T(2,128)(2,1)} all-to-all(bf16[8,2,49152]{2,1,0:T(2,128)(2,1)} %reshape.1024), channel_id=1, replica_groups=mesh['dp'=4,'seq'=8] {'seq'}, dimensions={0} | all-to-all | bytes 3145728 | tf_op jit(solution)/shard_map/all_to_all | solution.py:197
  601.3 13.9 fusion.5
  641.0 10.6 fusion.131
  676.3 13.4 reduce.55
  695.6 10.5 bitcast_add_fusion
  729.1 30.1 %copy.642 = bf16[1,2048,384]{2,0,1:T(2,128)(2,1)S(1)} copy(bf16[1,2048,384]{2,1,0:T(8,128)(2,1)S(1)} %fusion.39) | data formatting | bytes 3145728 | tf_op jit(solution)/shard_map/transpose(jvp(vmap(jit(_pad))))/pad | solution.py:16
  759.2 34.6 %reduce.56 = bf16[2048,384]{1,0:T(8,128)(2,1)} reduce(bf16[2048,1,384]{2,1,0:T(2,128)(2,1)S(1)} %bitcast.486, bf16[]{:T(256)} %broadcast.508), dimensions={1}, to_apply=%bitcast.467.reduce_sub_computation | reduce | bytes 3145730
  804.6 55.7 %all-to-all-done.4 = bf16[8,2,49152]{2,1,0:T(2,128)(2,1)} async-done(((bf16[8,2,49152]{2,1,0:T(2,128)(2,1)}), bf16[8,2,49152]{2,1,0:T(2,128)(2,1)}, u32[]{:S(2)}, u32[]{:S(2)}) %all-to-all-start.4) | async-done | bytes 1572896 | tf_op jit(solution)/shard_map/all_to_all | solution.py:200
  870.2 12.9 fusion.71
  886.5 17.3 %fusion.18 = f32[32,48,6448]{2,1,0:T(8,128)} fusion(bf16[32,48,256]{2,1,0:T(8,128)(2,1)S(1)} %bitcast.512, bf16[1,256,48]{1,2,0:T(8,128)(2,1)S(1)} %all_to_all.71, bf16[1,256,256]{1,2,0:T(8,128)(2,1)S(1)} %convert_element_type.201, bf16[1,256,3072]{1,2,0:T(8,128)(2,1)} %bitcast.501, bf16[1,256,3072]{1,2,0:T(8,128)(2,1)S(1)} %copy-done.25), kind=kOutput, calls=%fused_computation.33 | convolution fusion | flops 5084119040 | bytes 43704320 | tf_op jit(solution)/shard_map/hrx,hrw->xw/dot_general | solution.py:212
  908.5 361.2 %reduce-scatter.6.cloned.1.call-done = f32[1,48,6448]{2,1,0:T(8,128)} async-done(((f32[32,48,6448]{2,1,0:T(8,128)}), f32[1,48,6448]{2,1,0:T(8,128)}) %reduce-scatter.6.cloned.1.call-update) | async-done | bytes 1238032 | tf_op jit(solution)/shard_map/reduce_scatter | solution.py:259
  1269.7 7.4 fusion.51
  1277.1 126.4 %all-reduce.27.cloned.1.call-done = (f32[32,48]{1,0:T(8,128)}, f32[4,3072]{1,0:T(4,128)}, f32[3072]{0:T(1024)}, f32[4,256]{1,0:T(4,128)}, f32[256]{0:T(256)}, /*...) async-done(((f32[32,48]{1,0:T(8,128)}, f32[4,3072]{1,0:T(4,128)}, f32[3072]{0:T(1024)}, f32[4,256]{1,0:T(4,128)}, f32[256]{0:T(256)}, ...) | async-done | bytes 85584
  1404.2 12.5 all-gather.2
  1419.3 9.1 all-gather.3
  1429.7 27.8 %all-gather.18.cloned.1.call-done = f32[8,96,1536]{2,1,0:T(8,128)} async-done(((f32[1,96,1536]{2,1,0:T(8,128)}), f32[8,96,1536]{2,1,0:T(8,128)}) %all-gather.18.cloned.1.call-update) | async-done | bytes 4718608 | tf_op jit(solution)/shard_map/all_gather | solution.py:267
  1457.5 96.0 %all-gather.16.cloned.1.call-done = f32[8,48,6448]{2,1,0:T(8,128)} async-done(((f32[1,48,6448]{2,1,0:T(8,128)}), f32[8,48,6448]{2,1,0:T(8,128)}) %all-gather.16.cloned.1.call-update) | async-done | bytes 9904144 | tf_op jit(solution)/shard_map/all_gather | solution.py:265
  1553.6 10.7 copy.484
  (335 shorter events, 257.6 us)
Async XLA Ops:
  7.2 188.8 %all-gather.10.cloned.1.call-start = ((), (), s32[]{:S(2)}) async-start(), calls=%async_computation.9 | async-start | bytes 24760320 | tf_op jit(solution)/shard_map/all_gather | solution.py:124
  7.9 255.2 %all-gather.12.cloned.1.call-start = ((), (), s32[]{:S(2)}) async-start(), calls=%async_computation.10 | async-start | bytes 1179648 | tf_op jit(solution)/shard_map/all_gather | solution.py:146
  17.6 188.3 %copy-start.30 = (f32[1536]{0:T(1024)}, f32[1536]{0:T(1024)S(1)}, u32[]{:S(2)}) copy-start(f32[1536]{0:T(1024)S(1)} %reshape.975) | copy-start | bytes 18436
  17.9 188.1 %copy-start.44 = (f32[256]{0:T(256)}, f32[256]{0:T(256)S(1)}, u32[]{:S(2)}) copy-start(f32[256]{0:T(256)S(1)} %add_rsqrt_fusion.1) | copy-start | bytes 3076
  206.7 280.7 %all-gather.14.cloned.1.call-start = ((), (), s32[]{:S(2)}) async-start(), calls=%async_computation.11 | async-start | bytes 11796480 | tf_op jit(solution)/shard_map/all_gather | solution.py:171
  209.4 42.8 %all-to-all-start.1 = ((bf16[8,2,768]{2,1,0:T(2,128)(2,1)}), bf16[8,2,768]{2,1,0:T(2,128)(2,1)S(1)}, u32[]{:S(2)}, u32[]{:S(2)}) async-start(bf16[8,2,768]{2,1,0:T(2,128)(2,1)} %reshape.1020), calls=%async_computation.1 | async-start | bytes 49152 | tf_op jit(solution)/shard_map/all_to_all | solution.py:144
  214.1 43.8 %copy-start.46 = (pred[8,8]{1,0:T(8,128)(4,1)}, pred[8,8]{1,0:T(8,128)(4,1)S(1)}, u32[]{:S(2)}) copy-start(pred[8,8]{1,0:T(8,128)(4,1)S(1)} %iota_compare_fusion.6) | copy-start | bytes 196
  248.5 12.7 copy-start.53
  252.2 12.3 copy-start.56
  252.2 43.3 %all-to-all-start = ((bf16[8,2,49152]{2,1,0:T(2,128)(2,1)}), bf16[8,2,49152]{2,1,0:T(2,128)(2,1)}, u32[]{:S(2)}, u32[]{:S(2)}) async-start(bf16[8,2,49152]{2,1,0:T(2,128)(2,1)} %reshape.1018), calls=%async_computation | async-start | bytes 3145728 | tf_op jit(solution)/shard_map/all_to_all | solution.py:143
  257.9 400.5 %copy-start.42 = (f32[6]{0:T(128)}, f32[6]{0:T(128)S(1)}, u32[]{:S(2)}) copy-start(f32[6]{0:T(128)S(1)} %dynamic_slice.17) | copy-start | bytes 76
  260.5 44.4 %copy-start.38 = (f32[384]{0:T(512)}, f32[384]{0:T(512)S(1)}, u32[]{:S(2)}) copy-start(f32[384]{0:T(512)S(1)} %get-tuple-element.127) | copy-start | bytes 4612
  315.8 11.5 copy-start
  327.3 15.2 copy-start.12
  425.7 42.1 %all-to-all-start.2 = ((bf16[8,2,49152]{2,1,0:T(2,128)(2,1)}), bf16[8,2,49152]{2,1,0:T(2,128)(2,1)}, u32[]{:S(2)}, u32[]{:S(2)}) async-start(bf16[8,2,49152]{2,1,0:T(2,128)(2,1)} %reshape.1022), calls=%async_computation.2 | async-start | bytes 3145728 | tf_op jit(solution)/shard_map/all_to_all | solution.py:169
  430.0 439.2 %reduce-scatter.4.cloned.1.call-start = ((), (), s32[]{:S(2)}) async-start(), calls=%async_computation.12 | async-start | bytes 2359296 | tf_op jit(solution)/shard_map/reduce_scatter | solution.py:207
  595.8 19.3 %copy-start.8 = (f32[6,128,64,8]{1,2,0,3:T(8,128)}, f32[6,128,64,8]{1,2,0,3:T(8,128)S(1)}, u32[]{:S(2)}) copy-start(f32[6,128,64,8]{1,2,0,3:T(8,128)S(1)} %fusion.78) | copy-start | bytes 4718596
  640.8 267.0 %reduce-scatter.8.cloned.1.call-start = ((), (), s32[]{:S(2)}) async-start(), calls=%async_computation.15 | async-start | bytes 19464192 | tf_op jit(solution)/shard_map/reduce_scatter | solution.py:261
  692.1 105.5 %all-to-all-start.5 = ((bf16[8,2,768]{2,1,0:T(2,128)(2,1)}), bf16[8,2,768]{2,1,0:T(2,128)(2,1)S(1)}, u32[]{:S(2)}, u32[]{:S(2)}) async-start(bf16[8,2,768]{2,1,0:T(2,128)(2,1)} %reshape.1026), calls=%async_computation.6 | async-start | bytes 49152 | tf_op jit(solution)/shard_map/all_to_all | solution.py:203
  797.6 62.7 %all-to-all-start.4 = ((bf16[8,2,49152]{2,1,0:T(2,128)(2,1)}), bf16[8,2,49152]{2,1,0:T(2,128)(2,1)}, u32[]{:S(2)}, u32[]{:S(2)}) async-start(bf16[8,2,49152]{2,1,0:T(2,128)(2,1)} %reshape.1028), calls=%async_computation.4 | async-start | bytes 3145728 | tf_op jit(solution)/shard_map/all_to_all | solution.py:200
  802.7 467.0 %reduce-scatter.6.cloned.1.call-start = ((), (), s32[]{:S(2)}) async-start(), calls=%async_computation.13 | async-start | bytes 41361408 | tf_op jit(solution)/shard_map/reduce_scatter | solution.py:259
  870.2 12.9 copy-start.26
  903.8 365.9 %copy-start.4 = (bf16[1,256,3072]{1,2,0:T(8,128)(2,1)S(1)}, bf16[1,256,3072]{1,2,0:T(8,128)(2,1)}, u32[]{:S(2)}) copy-start(bf16[1,256,3072]{1,2,0:T(8,128)(2,1)} %get-tuple-element.151) | copy-start | bytes 4718596
  903.9 499.7 %all-reduce.27.cloned.1.call-start = ((), (), s32[]{:S(2)}) async-start(), calls=%async_computation.17 | async-start | bytes 201728
  907.7 549.8 %all-gather.18.cloned.1.call-start = ((), (), s32[]{:S(2)}) async-start(), calls=%async_computation.16 | async-start | bytes 5308416 | tf_op jit(solution)/shard_map/all_gather | solution.py:267
  908.4 645.1 %all-gather.16.cloned.1.call-start = ((), (), s32[]{:S(2)}) async-start(), calls=%async_computation.14 | async-start | bytes 11280384 | tf_op jit(solution)/shard_map/all_gather | solution.py:265
  1553.5 11.4 copy-start.41
  1553.5 12.0 copy-start.54
  1553.5 12.5 copy-start.58
  1553.5 13.1 copy-start.69
  1553.5 13.6 copy-start.68
  1553.6 14.1 copy-start.67
  (55 other events, 247.8 us)
Sparse Core Ops, SparseCore 0:
  9.9 186.0 all-gather.9
  206.8 24.2 all-gather.11
  233.0 94.6 all-gather.13
  640.9 34.0 reduce-scatter.3
  681.2 219.5 reduce-scatter.7
  907.0 362.5 reduce-scatter.5
  1277.2 126.2 all-reduce.26
  1405.2 52.2 all-gather.17
  1459.2 94.3 all-gather.15
where the time goes:
time: 1590 us; the launch traced here: 1580 us
  waiting for transfers between devices  897 us (56%)
  local copies, waits for them, and re-layouts  233 us (15%)
  other arithmetic  176 us (11%)
  matrix products  153 us (10%)
  blocking collectives  81.9 us (5%)
  starting transfers between devices  23.5 us (1%)
    reduce_scatter x1, waiting for transfers between devices, on_device(): lax.psum_scatter(grad_parts[0], ('dp', 'seq'), scatter_dimension=0, tiled...  361 us
    all_gather x1, waiting for transfers between devices, on_device(): lax.all_gather(in_weight, 'dp', axis=0, tiled=True)  178 us
    unnamed x10, waiting for transfers between devices  129 us
    unnamed x7, other arithmetic  122 us
    all_gather x1, waiting for transfers between devices, on_device(): lax.all_gather(own_rows[0], 'seq', axis=0, tiled=True)  96 us
    unnamed x178, local copies, waits for them, and re-layouts  74.1 us
    all_to_all x1, waiting for transfers between devices, on_device(): lax.all_to_all(pulled[0].astype(jnp.bfloat16), 'seq', split_axis=1, conca...  55.7 us
    all_to_all x1, blocking collectives, on_device(): lax.all_to_all(grad_y, 'seq', split_axis=2, concat_axis=1, tiled=True)  42.6 us
  transfers between devices with their start and end apart: 14, of which 8 were waited for; matrix products, arithmetic and copies ran while one was open for 26% of the time, Pallas kernels for 0%

commit v1 on v0

v1 whole, which is shorter than its diff:
```python
import functools

import jax
import jax.numpy as jnp
from jax import lax
from jax.experimental import pallas as pl
from jax.experimental.pallas import tpu as pltpu
from jax.sharding import Mesh
from jax.sharding import PartitionSpec as P

EPSILON = 1e-05
BLOCK = 256
HALO = 16
F32 = jnp.float32
BF16 = jnp.bfloat16
NN = ((1,), (0,))
NT = ((1,), (1,))
TN = ((0,), (0,))


def mm(a, b, dims=NN):
    return lax.dot_general(
        a.astype(BF16), b.astype(BF16), (dims, ((), ())), preferred_element_type=F32
    )


def split(a):
    high = a.astype(BF16)
    return high, (a - high.astype(F32)).astype(BF16)


def mm3(a, b, dims=NN):
    ah, al = split(a)
    bh, bl = split(b)
    return mm(ah, bh, dims) + (mm(ah, bl, dims) + mm(al, bh, dims))


def mm_exact(a, b, dims=NN):
    b0 = b.astype(BF16)
    r1 = b - b0.astype(F32)
    b1 = r1.astype(BF16)
    b2 = (r1 - b1.astype(F32)).astype(BF16)
    return mm(a, b0, dims) + (mm(a, b1, dims) + mm(a, b2, dims))


def mm_sum(a, b, dims=NN):
    ah, al = split(a)
    return mm(ah, b, dims) + mm(al, b, dims)


def sigmoid(v):
    return 1.0 / (1.0 + jnp.exp(-v))


def lane_mask(width, first):
    lane = lax.broadcasted_iota(jnp.int32, (1, 128), 1)
    return (lane < 64) if first else (lane >= 64)


def expand(v, pair):
    lane = lax.broadcasted_iota(jnp.int32, (1, 128), 1)
    return jnp.where(lane < 64, v[:, 2 * pair : 2 * pair + 1], v[:, 2 * pair + 1 : 2 * pair + 2])


def lower_mask():
    return lax.broadcasted_iota(jnp.int32, (BLOCK, BLOCK), 0) >= lax.broadcasted_iota(
        jnp.int32, (BLOCK, BLOCK), 1
    )


def head_indicator(pair):
    row = lax.broadcasted_iota(jnp.int32, (128, 128), 0)
    col = lax.broadcasted_iota(jnp.int32, (128, 128), 1)
    return (col == 2 * pair + row // 64).astype(BF16)


def conv_block(p_ref, row, col, w_ref, b_ref, wcol):
    raw = p_ref[pl.ds(row, BLOCK + HALO), col : col + 128].astype(F32)
    shifted = [raw[HALO - 3 + k : HALO - 3 + k + BLOCK] for k in range(4)]
    pre = b_ref[0:1, wcol : wcol + 128]
    for k in range(4):
        pre = pre + w_ref[k : k + 1, wcol : wcol + 128] * shifted[k]
    return pre, shifted


def prep_kernel(
    width, px_ref, pt_ref, pd_ref, wx_ref, bx_ref, wb_ref, bb_ref, dtb_ref, alog_ref,
    xs_ref, bc_ref, dt_ref, cum_ref, fin_ref,
):
    blocks = xs_ref.shape[0] // BLOCK
    rate = -jnp.exp(alog_ref[...])
    fin_ref[...] = jnp.zeros_like(fin_ref)

    def step(b, carry):
        row = pl.multiple_of(b * BLOCK, BLOCK)
        for c in range(2):
            pre, _ = conv_block(pt_ref, row, 128 * c, wb_ref, bb_ref, 128 * c)
            bc_ref[pl.ds(row, BLOCK), 128 * c : 128 * c + 128] = pre * sigmoid(pre)
        raw = pd_ref[pl.ds(row + HALO, BLOCK), :].astype(F32)
        raw = raw + dtb_ref[...]
        dt = jnp.maximum(raw, 0.0) + jnp.log1p(jnp.exp(-jnp.abs(raw)))
        cum = mm_exact(lower_mask().astype(F32), dt * rate)
        dt_ref[pl.ds(row, BLOCK), :] = dt
        cum_ref[pl.ds(row, BLOCK), :] = cum
        last = cum[BLOCK - 1 : BLOCK, :]
        weight = dt * jnp.exp(last - cum)
        decay = jnp.exp(last)
        keys_t = bc_ref[pl.ds(row, BLOCK), 0:128].T
        for pair in range(width // 128):
            cols = slice(128 * pair, 128 * pair + 128)
            pre, _ = conv_block(px_ref, row, 128 * pair, wx_ref, bx_ref, 128 * pair)
            xs = pre * sigmoid(pre)
            xs_ref[pl.ds(row, BLOCK), cols] = xs
            fin_ref[:, cols] = fin_ref[:, cols] * expand(decay, pair) + mm3(
                keys_t, xs * expand(weight, pair)
            )
        return carry

    lax.fori_loop(0, blocks, step, 0)


def forward_kernel(
    width, xs_ref, bc_ref, dt_ref, cum_ref, enter_ref, skip_ref, y_ref, yl_ref, states_ref, s_ref
):
    blocks = xs_ref.shape[0] // BLOCK
    s_ref[...] = enter_ref[...].astype(F32)

    def step(b, carry):
        row = pl.multiple_of(b * BLOCK, BLOCK)
        rows = pl.ds(row, BLOCK)
        dt, cum = dt_ref[rows, :], cum_ref[rows, :]
        cum_t = cum.T
        last = cum[BLOCK - 1 : BLOCK, :]
        grow, decay = jnp.exp(cum), jnp.exp(last)
        weight = dt * jnp.exp(last - cum)
        keys, queries = bc_ref[rows, 0:128], bc_ref[rows, 128:256]
        scores = mm3(queries, keys, NT)
        keys_t = keys.T
        mask = lower_mask()
        for pair in range(width // 128):
            cols = slice(128 * pair, 128 * pair + 128)
            xs = xs_ref[rows, cols]
            stepped = xs * expand(dt, pair)
            state = s_ref[:, cols]
            states_ref[b, :, cols] = state
            y = expand(grow, pair) * mm3(queries, state)
            for half in range(2):
                h = 2 * pair + half
                spread = cum[:, h : h + 1] - cum_t[h : h + 1, :]
                table = jnp.exp(jnp.where(mask, spread, -1e30))
                part = jnp.where(lane_mask(128, half == 0), stepped, 0.0)
                y = y + mm3(scores * table, part)
            s_ref[:, cols] = state * expand(decay, pair) + mm3(keys_t, xs * expand(weight, pair))
            yl_ref[rows, cols] = y
            y_ref[rows, cols] = (y + skip_ref[0:1, cols] * xs).astype(BF16)
        return carry

    lax.fori_loop(0, blocks, step, 0)


def leave_kernel(width, bc_ref, cum_ref, gy_ref, out_ref):
    blocks = gy_ref.shape[0] // BLOCK
    out_ref[...] = jnp.zeros_like(out_ref)

    def step(i, carry):
        row = pl.multiple_of((blocks - 1 - i) * BLOCK, BLOCK)
        rows = pl.ds(row, BLOCK)
        cum = cum_ref[rows, :]
        grow, decay = jnp.exp(cum), jnp.exp(cum[BLOCK - 1 : BLOCK, :])
        queries_t = bc_ref[rows, 128:256].T
        for pair in range(width // 128):
            cols = slice(128 * pair, 128 * pair + 128)
            dy = gy_ref[rows, cols].astype(F32)
            out_ref[:, cols] = out_ref[:, cols] * expand(decay, pair) + mm3(
                queries_t, expand(grow, pair) * dy
            )
        return carry

    lax.fori_loop(0, blocks, step, 0)


def backward_kernel(
    width, px_ref, pt_ref, pd_ref, xs_ref, bc_ref, dt_ref, cum_ref, gy_ref, yl_ref, states_ref, ds_in_ref, skip_ref,
    wx_ref, bx_ref, wb_ref, bb_ref, dtb_ref, alog_ref,
    dpre_ref, dpb_ref, gdt_ref, gwx_ref, gwb_ref, head_ref,
    ds_ref, dscore_ref,
):
    blocks = gy_ref.shape[0] // BLOCK
    rate = -jnp.exp(alog_ref[...])
    ds_ref[...] = ds_in_ref[...].astype(F32)
    gwx_ref[...] = jnp.zeros_like(gwx_ref)
    gwb_ref[...] = jnp.zeros_like(gwb_ref)
    head_ref[...] = jnp.zeros_like(head_ref)

    def step(i, carry):
        b = blocks - 1 - i
        row = pl.multiple_of(b * BLOCK, BLOCK)
        rows = pl.ds(row, BLOCK)
        dt, cum = dt_ref[rows, :], cum_ref[rows, :]
        cum_t = cum.T
        last = cum[BLOCK - 1 : BLOCK, :]
        grow, decay, tail = jnp.exp(cum), jnp.exp(last), jnp.exp(last - cum)
        keys, queries = bc_ref[rows, 0:128], bc_ref[rows, 128:256]
        scores = mm3(queries, keys, NT)
        queries_t = queries.T
        mask = lower_mask()
        dscore_ref[...] = jnp.zeros_like(dscore_ref)
        dkeys = jnp.zeros((BLOCK, 128), F32)
        dqueries = jnp.zeros((BLOCK, 128), F32)
        dcum = jnp.zeros((BLOCK, 128), F32)
        ddt = jnp.zeros((BLOCK, 128), F32)
        dlast = jnp.zeros((1, 128), F32)
        for pair in range(width // 128):
            cols = slice(128 * pair, 128 * pair + 128)
            xs = xs_ref[rows, cols]
            dt_e = expand(dt, pair)
            stepped_f = xs * dt_e
            stepped, stepped_low = split(stepped_f)
            dy = gy_ref[rows, cols]
            dy_f = dy.astype(F32)
            state, ds = states_ref[b, :, cols], ds_ref[:, cols]
            dstep = jnp.zeros((BLOCK, 128), F32)
            for half in range(2):
                h = 2 * pair + half
                spread = cum[:, h : h + 1] - cum_t[h : h + 1, :]
                table = jnp.exp(jnp.where(mask, spread, -1e30))
                part = jnp.where(lane_mask(128, half == 0), dy_f, 0.0).astype(BF16)
                dmix = mm(part, stepped, NT) + mm(part, stepped_low, NT)
                dscore_ref[...] += dmix * table
                high, low = split(scores * table)
                dstep = dstep + (mm(high, part, TN) + mm(low, part, TN))
            tail_e = expand(tail, pair)
            carried = mm3(keys, ds) * tail_e
            dstep = dstep + carried
            dkeys = dkeys + mm3(xs * dt_e * tail_e, ds, NT)
            grown = expand(grow, pair) * dy_f
            dqueries = dqueries + mm3(grown, state, NT)
            decay_e = expand(decay, pair)
            ends = jnp.sum(stepped_f * carried, 0, keepdims=True) + decay_e * jnp.sum(
                ds * state, 0, keepdims=True
            )
            ds_ref[:, cols] = ds * decay_e + mm3(queries_t, grown)
            dxs = dstep * dt_e + skip_ref[0:1, cols] * dy_f
            which = head_indicator(pair)
            ddt = ddt + mm_sum(dstep * xs, which)
            dcum = dcum + mm_sum(dy_f * yl_ref[rows, cols] - stepped_f * dstep, which)
            dlast = dlast + mm_sum(jnp.broadcast_to(ends, (8, 128)), which)[0:1]
            pre, shifted = conv_block(px_ref, row, 128 * pair, wx_ref, bx_ref, 128 * pair)
            sig = sigmoid(pre)
            dpre = dxs * sig * (1.0 + pre * (1.0 - sig))
            dpre_ref[rows, cols] = dpre
            for k in range(4):
                gwx_ref[k : k + 1, cols] += jnp.sum(dpre * shifted[k], 0, keepdims=True)
            gwx_ref[4:5, cols] += jnp.sum(dpre, 0, keepdims=True)
            gwx_ref[5:6, cols] += jnp.sum(dy_f * xs, 0, keepdims=True)
        at_end = lax.broadcasted_iota(jnp.int32, (BLOCK, 128), 0) == BLOCK - 1
        dcum = dcum + jnp.where(at_end, dlast, 0.0)
        dlog = mm_exact(mask.astype(F32), dcum, TN)
        raw = pd_ref[pl.ds(row + HALO, BLOCK), :].astype(F32)
        draw = (ddt + dlog * rate) * sigmoid(raw + dtb_ref[...])
        gdt_ref[rows, :] = draw
        head_ref[0:1, :] += jnp.sum(draw, 0, keepdims=True)
        head_ref[1:2, :] += jnp.sum(dlog * dt, 0, keepdims=True) * rate
        dqueries = dqueries + mm3(dscore_ref[...], keys)
        dkeys = dkeys + mm3(dscore_ref[...], queries, TN)
        for c, grad in enumerate((dkeys, dqueries)):
            cols = slice(128 * c, 128 * c + 128)
            pre, shifted = conv_block(pt_ref, row, 128 * c, wb_ref, bb_ref, 128 * c)
            sig = sigmoid(pre)
            dpre = grad * sig * (1.0 + pre * (1.0 - sig))
            dpb_ref[rows, cols] = dpre
            for k in range(4):
                gwb_ref[k : k + 1, cols] += jnp.sum(dpre * shifted[k], 0, keepdims=True)
            gwb_ref[4:5, cols] += jnp.sum(dpre, 0, keepdims=True)
        return carry

    lax.fori_loop(0, blocks, step, 0)


MESH = pl.DeviceIdType.MESH


def bits_of(count):
    return [1 << i for i in range(count.bit_length() - 1)]


def bit_at(index, bit):
    return (index // bit) % 2


def flip(index, bits):
    for bit in bits:
        index = index + bit * (1 - 2 * bit_at(index, bit))
    return index


def subsets(bits):
    found = [frozenset()]
    for bit in bits:
        found = found + [f | {bit} for f in found]
    return found


class Links:
    def __init__(self, send, recv):
        self.send, self.recv, self.count, self.open = send, recv, 0, []

    def make(self, src, dst, target, index=None):
        if index is None:
            index, self.count = self.count, self.count + 1
        return pltpu.make_async_remote_copy(
            src_ref=src, dst_ref=dst, send_sem=self.send.at[index], recv_sem=self.recv.at[index],
            device_id=target, device_id_type=MESH,
        )

    def start(self, src, dst, target):
        copy = self.make(src, dst, target)
        copy.start()
        self.open.append(copy)
        return copy

    def drain(self):
        for copy in self.open:
            copy.wait_send()


def meet(targets):
    barrier = pltpu.get_barrier_semaphore()
    for target in targets:
        pl.semaphore_signal(barrier, inc=1, device_id=target, device_id_type=MESH)
    pl.semaphore_wait(barrier, len(targets))


def neighbours(axis):
    me = lax.axis_index(axis)
    return [{axis: flip(me, (bit,))} for bit in bits_of(lax.axis_size(axis))]


def run_flows(flows):
    flows = list(flows)
    while flows:
        flows = [flow for flow in flows if next(flow, flow) is not flow]


def add_rows(out, a, b):
    rows = out.shape[0]
    step = 16 if rows % 16 == 0 else 8

    @pl.loop(0, rows // step)
    def _(i):
        at = pl.ds(pl.multiple_of(i * step, step), step)
        out[at, :] = (a[at, :].astype(F32) + b[at, :].astype(F32)).astype(out.dtype)


def gather_flow(links, axis, order, own, slot):
    me = lax.axis_index(axis)
    held = [frozenset()]
    for bit in order:
        target = {axis: flip(me, (bit,))}
        copies = [
            links.start(slot(flip(me, f)) if f else own, slot(flip(me, f)), target) for f in held
        ]
        yield None
        for copy in copies:
            copy.wait_recv()
        held = held + [f | {bit} for f in held]


def reduce_flow(links, axis, order, source, inbox, total, final=None):
    me = lax.axis_index(axis)
    base = 0

    def current(f):
        return source(flip(me, f))

    for stage, bit in enumerate(order):
        keep = subsets(order[stage + 1 :])
        target = {axis: flip(me, (bit,))}
        copies = [
            links.start(current(f | {bit}), inbox(base + k), target) for k, f in enumerate(keep)
        ]
        yield None
        places = {}
        for k, f in enumerate(keep):
            copies[k].wait_recv()
            out = total(base + k)
            if final is not None and stage == len(order) - 1:
                out = final
            add_rows(out, current(f), inbox(base + k))
            places[f] = out
        current = places.__getitem__
        base += len(keep)


def spread_flow(links, order, block):
    d, q = lax.axis_index("dp"), lax.axis_index("quad")
    away = {bit: bit_at(d, bit) != bit_at(q, bit) for bit in order}
    for stage, bit in enumerate(order):
        reached = jnp.bool_(True)
        for later in order[stage + 1 :]:
            reached = jnp.logical_and(reached, jnp.logical_not(away[later]))
        holder = jnp.logical_and(reached, jnp.logical_not(away[bit]))
        taker = jnp.logical_and(reached, away[bit])
        index, links.count = links.count, links.count + 1
        target = {"dp": flip(d, (bit,))}

        @pl.when(holder)
        def _():
            links.make(block, block, target, index).start()

        yield None

        @pl.when(holder)
        def _():
            links.make(block, block, target, index).wait_send()

        @pl.when(taker)
        def _():
            links.make(block, block, target, index).wait_recv()


def collect_kernel(
    width, win_ref, wt_ref, wo_in_ref, hid_ref, og_ref, gain_ref,
    wz_ref, wx_ref, wt_out, wo_ref, hid_out, og_out, gain_out, halo_ref, send, recv, local,
):
    d, q, p = lax.axis_index("dp"), lax.axis_index("quad"), lax.axis_index("pair")
    rows = win_ref.shape[0]
    inner = width * lax.axis_size("quad")
    links = Links(send, recv)
    dp_bits, quad_bits = bits_of(lax.axis_size("dp")), bits_of(lax.axis_size("quad"))
    meet(neighbours("dp") + neighbours("quad") + neighbours("pair"))

    def columns(base):
        return pl.ds(pl.multiple_of(base + q * width, 128), width)

    flows = [gather_flow(links, "dp", dp_bits, gain_ref, lambda i: gain_out.at[i])]

    def weights(source, out):
        for h, order in enumerate((dp_bits, dp_bits[::-1])):
            part = pl.ds(h * (rows // 2), rows // 2)
            flows.append(
                gather_flow(links, "dp", order, source(part), lambda i, part=part: out.at[i, part])
            )

    weights(lambda part: win_ref.at[part, columns(inner)], wx_ref)
    weights(lambda part: wt_ref.at[part], wt_out)
    flows.append(gather_flow(links, "quad", quad_bits[::-1], hid_ref, lambda i: hid_out.at[i]))
    weights(lambda part: win_ref.at[part, columns(0)], wz_ref)
    flows.append(gather_flow(links, "quad", quad_bits[::-1], og_ref, lambda i: og_out.at[i]))
    owned = [
        (win_ref.at[:, columns(inner)], wx_ref.at[d]), (wt_ref, wt_out.at[d]),
        (win_ref.at[:, columns(0)], wz_ref.at[d]), (hid_ref, hid_out.at[q]),
        (og_ref, og_out.at[q]), (gain_ref, gain_out.at[d]),
    ]
    copies = [pltpu.make_async_copy(a, b, local.at[i]) for i, (a, b) in enumerate(owned)]

    @pl.when(d == q)
    def _():
        copy = pltpu.make_async_copy(wo_in_ref, wo_ref, local.at[len(owned)])
        copy.start()
        copy.wait()

    half = width // 2
    for h, order in enumerate((dp_bits, dp_bits[::-1])):
        flows.append(spread_flow(links, order, wo_ref.at[pl.ds(h * half, half)]))

    def halo():
        for _ in quad_bits:
            yield None
        tail = hid_out.at[hid_out.shape[0] - 1, pl.ds(hid_out.shape[1] - HALO, HALO)]
        copy = links.start(tail, halo_ref, {"pair": flip(p, (1,))})
        yield None
        copy.wait_recv()

    own_last = copies[3]
    for copy in copies:
        copy.start()
    own_last.wait()
    flows.append(halo())
    run_flows(flows)
    for copy in copies:
        if copy is not own_last:
            copy.wait()
    links.drain()


def combine_kernel(
    in_ref, out_ref, gn_ref, op_ref, small_ref,
    in_all, out_all, gn_own, op_own, small_all,
    in_box, in_sum, in_pair, out_box, out_sum, out_pair, out_tot, gn_box, gn_sum, op_box, op_sum,
    small_box, small_sum, send, recv,
):
    d, q, p = lax.axis_index("dp"), lax.axis_index("quad"), lax.axis_index("pair")
    links = Links(send, recv)
    dp_bits, quad_bits = bits_of(lax.axis_size("dp")), bits_of(lax.axis_size("quad"))
    blocks = lax.axis_size("dp") - 1
    near = neighbours("dp") + neighbours("quad") + neighbours("pair")
    swapped = {"dp": q, "quad": d}

    @pl.when(d == q)
    def _():
        meet(near)

    @pl.when(d != q)
    def _():
        meet([*near, swapped])

    other = {"pair": flip(p, (1,))}
    orders = (dp_bits, dp_bits[::-1])

    def in_flow(h):
        half = in_ref.shape[1] // 2
        part = pl.ds(h * half, half)
        yield from reduce_flow(
            links, "dp", orders[h], lambda i: in_ref.at[i, part],
            lambda k: in_box.at[h, k], lambda k: in_sum.at[h, k],
        )
        mine, box = in_sum.at[h, blocks - 1], in_pair.at[h]
        copy = links.start(mine, box, other)
        yield None
        copy.wait_recv()
        own = in_all.at[q, part]
        add_rows(own, mine, box)
        yield from gather_flow(
            links, "quad", quad_bits[::-1], own, lambda i: in_all.at[i, part]
        )

    def out_flow(h):
        half = out_ref.shape[2] // 2
        part = pl.ds(h * half, half)
        yield from reduce_flow(
            links, "dp", orders[h], lambda i: out_ref.at[i, :, part],
            lambda k: out_box.at[h, k], lambda k: out_sum.at[h, k],
        )
        mine, box, whole = out_sum.at[h, blocks - 1], out_pair.at[h], out_tot.at[h]
        copy = links.start(mine, box, other)
        yield None
        copy.wait_recv()
        add_rows(whole, mine, box)
        index, links.count = links.count, links.count + 1

        @pl.when(d == q)
        def _():
            out_all[q, :, part] = whole[...]

        @pl.when(d != q)
        def _():
            links.make(whole, out_all.at[d, :, part], swapped, index).start()

        yield None

        @pl.when(d != q)
        def _():
            links.make(whole, out_all.at[d, :, part], swapped, index).wait()

        yield from gather_flow(
            links, "quad", quad_bits[::-1], out_all.at[q, :, part], lambda i: out_all.at[i, :, part]
        )

    def small_flow():
        current = small_ref
        steps = [("dp", bit) for bit in dp_bits] + [("pair", 1)]
        for k, (axis, bit) in enumerate(steps):
            target = {axis: flip(lax.axis_index(axis), (bit,))}
            copy = links.start(current, small_box.at[k], target)
            yield None
            copy.wait_recv()
            out = small_sum.at[k] if k < len(steps) - 1 else small_all.at[q]
            out[...] = current[...] + small_box[k]
            current = out
        yield from gather_flow(
            links, "quad", quad_bits[::-1], small_all.at[q], lambda i: small_all.at[i]
        )

    run_flows([
        small_flow(),
        in_flow(0), in_flow(1),
        reduce_flow(
            links, "quad", quad_bits, lambda i: gn_ref.at[i], lambda k: gn_box.at[k],
            lambda k: gn_sum.at[k], gn_own,
        ),
        out_flow(0), out_flow(1),
        reduce_flow(
            links, "quad", quad_bits, lambda i: op_ref.at[i], lambda k: op_box.at[k],
            lambda k: op_sum.at[k], op_own,
        ),
    ])
    links.drain()


def remote_call(kernel, ident, outs, any_inputs, scratch, copies, extra=(), flops=10**6):
    vmem, anywhere = pl.BlockSpec(memory_space=pltpu.VMEM), pl.BlockSpec(memory_space=pl.ANY)

    def run(*args):
        moved = sum(a.size * a.dtype.itemsize for a in (*args, *outs))
        return pl.pallas_call(
            kernel,
            out_shape=tuple(outs),
            in_specs=[anywhere if i in any_inputs else vmem for i in range(len(args))],
            out_specs=tuple([vmem] * len(outs)),
            scratch_shapes=list(scratch)
            + [pltpu.SemaphoreType.DMA((copies,)), pltpu.SemaphoreType.DMA((copies,))]
            + list(extra),
            compiler_params=pltpu.CompilerParams(
                vmem_limit_bytes=62 * 2**20, collective_id=ident, has_side_effects=True
            ),
            cost_estimate=pl.CostEstimate(flops=flops, bytes_accessed=moved, transcendentals=0),
        )(*args)

    return run


def call(kernel, outs, scratch=(), flops=10**9):
    vmem = pl.BlockSpec(memory_space=pltpu.VMEM)

    def run(*args):
        moved = sum(a.size * a.dtype.itemsize for a in (*args, *outs))
        return pl.pallas_call(
            kernel,
            out_shape=tuple(outs),
            in_specs=[vmem] * len(args),
            out_specs=tuple([vmem] * len(outs)),
            scratch_shapes=list(scratch),
            compiler_params=pltpu.CompilerParams(vmem_limit_bytes=60 * 2**20),
            cost_estimate=pl.CostEstimate(flops=flops, bytes_accessed=moved, transcendentals=0),
        )(*args)

    return run


def on_device(
    hidden_in, pre_gain, in_weight, conv_x_weight, conv_x_bias, conv_bc_weight, conv_bc_bias,
    dt_bias, a_log, skip, norm_gain, out_weight, output_gradient,
):
    dp, pairs, quads = lax.axis_size("dp"), lax.axis_size("pair"), lax.axis_size("quad")
    pair_rank, quad = lax.axis_index("pair"), lax.axis_index("quad")
    _, local, model = hidden_in.shape
    inner = conv_x_bias.shape[0]
    state2 = conv_bc_bias.shape[0]
    heads = dt_bias.shape[0]
    width, own_heads, bc_cols = inner // quads, heads // quads, state2 // quads
    tokens = local * quads
    everyone = ("dp", "pair", "quad")

    def own(v, n, axis, base=0):
        return lax.dynamic_slice_in_dim(v, base + quad * n, n, axis)

    def sds(shape, dtype=F32):
        return jax.ShapeDtypeStruct(shape, dtype)

    pre_size = pre_gain.shape[0]
    gain_block = jnp.broadcast_to(jnp.concatenate([pre_gain, norm_gain]).astype(F32), (8, pre_size + norm_gain.shape[0]))
    w_tail = in_weight[:, 2 * inner :]
    tail_width = w_tail.shape[1] + -w_tail.shape[1] % 128
    w_tail = jnp.pad(w_tail, ((0, 0), (0, tail_width - w_tail.shape[1])))
    rows_dp = in_weight.shape[0]
    bits = len(bits_of(dp))
    copies = (dp - 1) * 7 + 2 * (quads - 1) + 2 * bits + 1
    wz, w_x, w_t, w_out, hidden_all, grad_all, gains, halo_rows = remote_call(
        functools.partial(collect_kernel, width), 0,
        [
            sds((dp, rows_dp, width), BF16), sds((dp, rows_dp, width), BF16),
            sds((dp, rows_dp, tail_width), BF16), sds((width, model), BF16),
            sds((quads, local, model), BF16), sds((quads, local, model), BF16),
            sds((dp, *gain_block.shape)), sds((HALO, model), BF16),
        ],
        range(6), [], copies, extra=[pltpu.SemaphoreType.DMA((7,))],
    )(in_weight, w_tail, out_weight, hidden_in[0], output_gradient[0], gain_block)
    pre_full = gains[:, 0, :pre_size].reshape(-1)
    norm_own = own(gains[:, 0, pre_size:].reshape(-1), width, 0)[None]
    wz, w_x = wz.reshape(model, width), w_x.reshape(model, width)
    w_t = w_t.reshape(model, tail_width)
    grad_all = grad_all.reshape(tokens, model)

    def unit(v):
        v = v.astype(F32)
        return v * lax.rsqrt(jnp.mean(v * v, -1, keepdims=True) + EPSILON)

    rows = hidden_in[0].astype(F32)
    inv_rms = lax.rsqrt(jnp.mean(rows * rows, -1, keepdims=True) + EPSILON)
    unit_rows = rows * inv_rms
    unit_all = unit(hidden_all.reshape(tokens, model))
    halo_unit = jnp.where(pair_rank > 0, unit(halo_rows), 0.0)
    normed_all = (unit_all * pre_full[None]).astype(BF16)
    normed_halo = jnp.concatenate([(halo_unit * pre_full[None]).astype(BF16), normed_all], 0)
    grad_rows = output_gradient[0]

    def project(v, w):
        return lax.optimization_barrier(jnp.dot(v, w, preferred_element_type=F32).astype(BF16))

    px, pt = project(normed_halo, w_x), project(normed_halo, w_t)
    gate = project(normed_all, wz).astype(F32)
    pd = jnp.pad(own(pt, own_heads, 1, state2), ((0, 0), (0, 128 - own_heads)))

    def pad_heads(v):
        return jnp.pad(own(v, own_heads, 0), (0, 128 - own_heads))[None]

    wx, bx = own(conv_x_weight, width, 1), own(conv_x_bias, width, 0)[None]
    wb, bb = conv_bc_weight, conv_bc_bias[None]
    dtb, alog = pad_heads(dt_bias), pad_heads(a_log)
    skip_own = jnp.repeat(own(skip, own_heads, 0), width // own_heads)[None]

    big, col = (tokens, width), (tokens, 128)
    xs, bc, dt, cum, final = call(
        functools.partial(prep_kernel, width),
        [sds(big), sds((tokens, state2)), sds(col), sds(col), sds((128, width))],
    )(px, pt, pd, wx, bx, wb, bb, dtb, alog)
    enter = lax.ppermute(final, "pair", [(i, i + 1) for i in range(pairs - 1)])
    y, y_long, states = call(
        functools.partial(forward_kernel, width),
        [sds(big, BF16), sds(big), sds((tokens // BLOCK, 128, width))],
        [pltpu.VMEM((128, width), F32)],
    )(xs, bc, dt, cum, enter, skip_own)

    y_float = y.astype(F32)
    sig = jax.nn.sigmoid(gate)
    gated = y_float * gate * sig
    grad_mixed = jnp.einsum("tf,cf->tc", grad_all, w_out, preferred_element_type=F32)
    grad_unit = grad_mixed * norm_own
    stats = lax.psum(
        jnp.stack([jnp.sum(gated * gated, -1), jnp.sum(grad_unit * gated, -1)]), "quad"
    )
    out_rms = lax.rsqrt(stats[0] / inner + EPSILON)[:, None]
    mean_dot = out_rms * stats[1][:, None] / inner
    unit_gated = gated * out_rms
    mixed = (unit_gated * norm_own).astype(BF16)
    norm_part = jnp.sum(grad_mixed * unit_gated, 0)
    grad_gated = out_rms * (grad_unit - unit_gated * mean_dot)
    grad_y = (grad_gated * gate * sig).astype(BF16)
    grad_gate = (grad_gated * y_float * sig * (1.0 + gate * (1.0 - sig))).astype(BF16)

    out_part = jnp.dot(mixed, w_out, preferred_element_type=F32).astype(BF16)

    leaving = call(functools.partial(leave_kernel, width), [sds((128, width))])(bc, cum, grad_y)[0]
    back = [(i + 1, i) for i in range(pairs - 1)]
    ds_in = lax.ppermute(leaving, "pair", back)
    dpre, dpb, gdt, gwx, gwb, heads_grad = call(
        functools.partial(backward_kernel, width),
        [sds(big), sds((tokens, state2)), sds(col), sds((8, width)), sds((8, state2)), sds((8, 128))],
        [pltpu.VMEM((128, width), F32), pltpu.VMEM((BLOCK, BLOCK), F32)],
    )(
        px, pt, pd, xs, bc, dt, cum, grad_y, y_long, states, ds_in, skip_own,
        wx, bx, wb, bb, dtb, alog,
    )
    after = lax.ppermute(jnp.concatenate([dpre[:8], dpb[:8]], 1), "pair", back)

    def unconv(v, tail, kernel):
        padded = jnp.concatenate([v, tail], 0)
        return sum(kernel[k][None] * padded[3 - k : 3 - k + tokens] for k in range(4))

    grad_x = unconv(dpre, after[:, :width], wx).astype(BF16)
    grad_bc = unconv(dpb, after[:, width:], wb)
    bc_local = lax.psum_scatter(grad_bc, "quad", scatter_dimension=0, tiled=True).astype(BF16)
    bc_all = lax.all_gather(bc_local, "quad", axis=0, tiled=True)
    tail_cols = jnp.concatenate(
        [own(bc_all, bc_cols, 1), gdt[:, :own_heads].astype(BF16)], 1
    )
    tail_pad = -(bc_cols + own_heads) % 128
    tail_cols = jnp.pad(tail_cols, ((0, 0), (0, tail_pad)))
    grad_proj = jnp.concatenate([grad_gate, grad_x, tail_cols], 1)
    w_tail_own = jnp.concatenate(
        [
            own(w_t, bc_cols, 1),
            own(w_t, own_heads, 1, state2),
        ],
        1,
    )
    w_tail_own = jnp.pad(w_tail_own, ((0, 0), (0, tail_pad)))
    nt = (((1,), (1,)), ((), ()))
    normed_part = (
        lax.dot_general(grad_gate, wz, nt, preferred_element_type=F32)
        + lax.dot_general(grad_x, w_x, nt, preferred_element_type=F32)
        + lax.dot_general(tail_cols, w_tail_own, nt, preferred_element_type=F32)
    )
    pre_part = jnp.sum(normed_part * unit_all, 0)
    in_part = jnp.einsum("tc,tp->cp", normed_all, grad_proj, preferred_element_type=F32)
    out_part_w = jnp.einsum("tc,tf->cf", mixed, grad_all, preferred_element_type=F32)
    norm_part = norm_part.reshape(-1, 128)
    small_in = jnp.concatenate(
        [
            gwx[:6].reshape(-1, 128), gwb[:5].reshape(-1, 128), heads_grad[:2],
            pre_part.reshape(-1, 128), norm_part,
        ],
        0,
    )
    small_rows = small_in.shape[0]
    small_in = jnp.pad(small_in, ((0, -small_rows % 8), (0, 0)))
    own_in, own_out = rows_dp, width // dp
    gw = grad_proj.shape[1]
    vm = pltpu.VMEM
    copies = 2 * (dp - 1 + 1 + quads - 1) + 2 * (dp - 1 + 2 + quads - 1) + 2 * (quads - 1) + bits + 1 + quads - 1
    in_all, out_all, gn_own, op_own, small_all = remote_call(
        combine_kernel, 1,
        [
            sds((quads, own_in, gw), BF16), sds((quads, own_out, model), BF16),
            sds((local, model)), sds((local, model)), sds((quads, *small_in.shape)),
        ],
        (),
        [
            vm((2, dp - 1, own_in // 2, gw), BF16), vm((2, dp - 1, own_in // 2, gw), BF16),
            vm((2, own_in // 2, gw), BF16),
            vm((2, dp - 1, own_out, model // 2), BF16), vm((2, dp - 1, own_out, model // 2), BF16),
            vm((2, own_out, model // 2), BF16), vm((2, own_out, model // 2), BF16),
            vm((quads - 1, local, model), BF16), vm((quads - 1, local, model), BF16),
            vm((quads - 1, local, model), BF16), vm((quads - 1, local, model), BF16),
            vm((bits + 1, *small_in.shape), F32), vm((bits + 1, *small_in.shape), F32),
        ],
        copies,
    )(
        in_part.astype(BF16).reshape(dp, own_in, gw), out_part_w.astype(BF16).reshape(dp, own_out, model),
        normed_part.astype(BF16).reshape(quads, local, model), out_part.reshape(quads, local, model),
        small_in,
    )
    output = rows + op_own
    normed_grad = gn_own
    unit_grad = normed_grad * pre_full[None]
    input_grad = grad_rows.astype(F32) + inv_rms * (
        unit_grad - unit_rows * jnp.mean(unit_grad * unit_rows, -1, keepdims=True)
    )
    cuts = (0, width, 2 * width, 2 * width + bc_cols, 2 * width + bc_cols + own_heads)
    in_weight_grad = jnp.concatenate(
        [in_all[q, :, lo:hi] for lo, hi in zip(cuts[:-1], cuts[1:]) for q in range(quads)], 1
    ).astype(F32)
    out_weight_grad = out_all.reshape(width, model).astype(F32)
    n_x, n_b = width // 128, state2 // 128
    at = 6 * n_x
    by_channel = small_all[:, :at].reshape(quads, 6, width)
    conv_x_grad = jnp.moveaxis(by_channel[:, :4], 0, 1).reshape(4, inner)
    conv_x_bias_grad = by_channel[:, 4].reshape(inner)
    skip_grad = by_channel[:, 5].reshape(heads, -1).sum(-1)
    summed = small_all.sum(0)
    bc_grad = summed[at : at + 5 * n_b].reshape(5, state2)
    at += 5 * n_b
    head_grad = jnp.moveaxis(small_all[:, at : at + 2, :own_heads], 0, 1).reshape(2, heads)
    at += 2
    pre_sum = summed[at : at + model // 128].reshape(-1)
    at += model // 128
    norm_sum = small_all[:, at : at + n_x].reshape(-1)
    rank = lax.axis_index("dp")
    return (
        output[None], input_grad[None],
        lax.dynamic_slice_in_dim(pre_sum, rank * (model // dp), model // dp, 0), in_weight_grad,
        conv_x_grad, conv_x_bias_grad, bc_grad[:4], bc_grad[4], head_grad[0], head_grad[1], skip_grad,
        lax.dynamic_slice_in_dim(norm_sum, rank * (inner // dp), inner // dp, 0), out_weight_grad,
    )


def solution(mesh):
    dp, seq = mesh.shape["dp"], mesh.shape["seq"]
    fine = Mesh(mesh.devices.reshape(dp, 2, seq // 2), ("dp", "pair", "quad"))
    tokens, whole, rows = P("dp", ("pair", "quad"), None), P(), P("dp", None)
    return jax.shard_map(
        on_device,
        mesh=fine,
        in_specs=(
            tokens, P("dp"), rows, whole, whole, whole, whole, whole, whole, whole, P("dp"), rows, tokens,
        ),
        out_specs=(
            tokens, tokens, P("dp"), rows, whole, whole, whole, whole, whole, whole, whole, P("dp"), rows,
        ),
        check_vma=False,
    )
```

time: 1590 us -> 597 us (0.38)
  waiting for transfers between devices: 897 us -> 13.7 us
  Pallas kernels: 0 us -> 353 us
  local copies, waits for them, and re-layouts: 233 us -> 82.4 us
  other arithmetic: 176 us -> 39.4 us
  matrix products: 153 us -> 63.1 us
  blocking collectives: 81.9 us -> 14.3 us
  starting transfers between devices: 23.5 us -> 7.22 us
    reduce_scatter x3 -> x1, waiting for transfers between devices: 361 us -> 0.01 us  [on_device(): lax.psum_scatter(grad_bc, 'quad', scatter_dimension=0, tiled=True)]
    pallas_call x0 -> x6, Pallas kernels: none -> 353 us  [the longest x2 286 us: run(): pl.pallas_call(kernel, out_shape=tuple(outs), in_specs=[anywhere if i in...]
    all_gather x5 -> x0, waiting for transfers between devices: 302 us -> none  [the longest x1 178 us: on_device(): lax.all_gather(in_weight, 'dp', axis=0, tiled=True)]
    unnamed x10 -> x1, waiting for transfers between devices: 129 us -> 0.02 us
    unnamed x7 -> x2, other arithmetic: 122 us -> 0.01 us
    all_to_all x5 -> x0, waiting for transfers between devices: 105 us -> none  [the longest x1 55.7 us: on_device(): lax.all_to_all(pulled[0].astype(jnp.bfloat16), 'seq', split_axis=1, conca...]
    dot_general x25 -> x10, matrix products: 153 us -> 63.1 us  [the longest x3 12.8 us: project(): jnp.dot(v, w, preferred_element_type=F32).astype(BF16)]
    convert_element_type x9 -> x0, local copies, waits for them, and re-layouts: 58.5 us -> none  [the longest x1 28.4 us: on_device(): y_heads = mixer_out.astype(jnp.bfloat16)]
  transfers between devices with their start and end apart: 14 -> 4, of which waited for: 8 -> 1; matrix products, arithmetic and copies ran while one was open for 26% -> 10% of each run, Pallas kernels for 0% -> 0%
where the time goes in v1:
time: 597 us; the launch traced here: 588 us
  Pallas kernels  353 us (59%)
  local copies, waits for them, and re-layouts  82.4 us (14%)
  matrix products  63.1 us (11%)
  other arithmetic  39.4 us (7%)
  between operations  15 us (3%)
  blocking collectives  14.3 us (2%)
  waiting for transfers between devices  13.7 us (2%)
  starting transfers between devices  7.22 us (1%)
    pallas_call x2, Pallas kernels, run(): pl.pallas_call(kernel, out_shape=tuple(outs), in_specs=[anywhere if i in...  286 us
    pallas_call x4, Pallas kernels, run(): pl.pallas_call(kernel, out_shape=tuple(outs), in_specs=[vmem] * len(args)...  67.3 us
    unnamed x67, local copies, waits for them, and re-layouts  19.6 us
    ppermute x1, waiting for transfers between devices, on_device(): ds_in = lax.ppermute(leaving, 'pair', back)  13.7 us
    dot_general x3, matrix products, project(): jnp.dot(v, w, preferred_element_type=F32).astype(BF16)  12.8 us
  transfers between devices with their start and end apart: 4, of which 1 were waited for; matrix products, arithmetic and copies ran while one was open for 10% of the time, Pallas kernels for 0%

profile of v1, /device:TPU:0, one launch (start us, length us, event | category | flops | bytes accessed | tf_op | source)
XLA Modules:
  0.0 588.3 jit_solution(8340770582122693019)
XLA Ops:
  11.4 7.5 %copy.33.win_ref = bf16[384,6448]{1,0:T(8,128)(2,1)} copy(bf16[384,6448]{0,1:T(8,128)(2,1)} %param.15) | data formatting | bytes 9904128 | tf_op args[2]
  21.3 102.3 %shard_map.228 = (bf16[4,384,768]{2,1,0:T(8,128)(2,1)}, bf16[4,384,768]{2,1,0:T(8,128)(2,1)}, bf16[4,384,384]{2,1,0:T(8,128)(2,1)}, bf16[768,1536]{1,0:T(8,128)(...) custom-call(bf16[384,6448]{1,0:T(8,128)(2,1)} %copy.33.win_ref, ...), custom_call_target="tpu_custom_call" | custom-call | flops 1000000 | bytes 23961600 | tf_op jit(solution)/shard_map/pallas_call | solution.py:596
  124.7 2.6 multiply_reduce_fusion.1
  131.2 2.7 convolution_convert_fusion.4.pt_ref
  135.8 6.4 %convolution_convert_fusion.3.px_ref = bf16[1040,768]{1,0:T(8,128)(2,1)} fusion(bf16[1536,768]{1,0:T(8,128)(2,1)} %bitcast.144, bf16[1024,1536]{1,0:T(8,128)(2,1)} %copy-done.4, bf16[16,1536]{1,0:T(8,128)(2,1)S(1)} %fusion.56), kind=kOutput, calls=%fused_computation.21 | convolution fusion | flops 2460856320 | bytes 7151616 | tf_op jit(solution)/shard_map/dot_general | solution.py:689
  142.7 11.1 %shard_map.229 = (f32[1024,768]{1,0:T(8,128)}, f32[1024,256]{1,0:T(8,128)}, f32[1024,128]{1,0:T(8,128)}, f32[1024,128]{1,0:T(8,128)}, f32[128,768]{1,0:T(8,128)}) custom-call(bf16[1040,768]{1,0:T(8,128)(2,1)} %convolution_convert_fusion.3.px_ref, bf16[1040,384]{1,0:T(8,128)(2,1)} %convolution_convert_fusion.4.pt_ref, bf16[1040,128]{1,0:T(8,128)(2,1)} %pad.28.pd_ref, ...), custom_call_target="tpu_custom_call" | custom-call | flops 1000000000 | bytes 8320000 | tf_op jit(solution)/shard_map/pallas_call | solution.py:618
  153.8 4.2 collective-permute-start
  168.4 3.7 convolution_convert_fusion.5
  174.9 2.0 constant_dynamic-slice_fusion.1
  176.8 16.4 %shard_map.230 = (bf16[1024,768]{1,0:T(8,128)(2,1)}, f32[1024,768]{1,0:T(8,128)}, f32[4,128,768]{2,1,0:T(8,128)}) custom-call(f32[1024,768]{1,0:T(8,128)} %get-tuple-element.45.xs_ref, f32[1024,256]{1,0:T(8,128)} %get-tuple-element.46.bc_ref, f32[1024,128]{1,0:T(8,128)} %get-tuple-element.47.dt_ref, f32[1024,128]{1,0:T(8,128)} %get-tuple-element.48.cum_ref, ...), custom_call_target="tpu_custom_call" | custom-call | flops 1000000000 | bytes 11930624 | tf_op jit(solution)/shard_map/pallas_call | solution.py:618
  193.2 8.3 %multiply_reduce_fusion.4 = (f32[1024]{0:T(1024)S(1)}, f32[1024]{0:T(1024)S(1)}, f32[1024,768]{1,0:T(8,128)}) fusion(bf16[1024,768]{1,0:T(8,128)(2,1)} %convolution_convert_fusion.5, bf16[1024,768]{1,0:T(8,128)(2,1)} %get-tuple-element.50, f32[768]{0:T(1024)S(1)} %dynamic_slice.42, bf16[1024,1536]{1,0:T(8,128)(2,1)} %bitcast.142, ...), kind=kOutput, calls=%fused_computation.47 | convolution fusion | flops 2425354240 | bytes 11807744 | tf_op jit(solution)/shard_map/tf,cf->tc/dot_general | solution.py:718
  202.2 7.8 %psum.7 = f32[2,1024]{1,0:T(2,128)} all-reduce(f32[2,1024]{1,0:T(2,128)} %pad_maximum_fusion.6), channel_id=1, replica_groups=mesh['dp'=4,'pair'=2,'quad'=4] {'quad'}, use_global_device_ids=true, to_apply=%region_4.5 | all-reduce | flops 2048 | bytes 16384 | tf_op jit(solution)/shard_map/psum | solution.py:720
  210.8 6.8 %fusion.7 = (bf16[1024,768]{1,0:T(8,128)(2,1)}, bf16[1024,768]{1,0:T(8,128)(2,1)}, f32[768]{0:T(1024)}) fusion(bf16[1024,768]{1,0:T(8,128)(2,1)} %get-tuple-element.50, bf16[1024,768]{1,0:T(8,128)(2,1)} %convolution_convert_fusion.5, f32[1024]{0:T(1024)S(1)} %multiply_multiply_fusion, f32[1024,768]{1,0:T(8,128)} %get-tuple-element.134, f32[768]{0:T(1024)} %copy-done.15, ...), kind=kLoop, calls=%fused_computation.25 | loop fusion | flops 18873600 | bytes 9451520 | tf_op jit(solution)/shard_map/convert_element_type | solution.py:730
  217.6 6.2 %shard_map.231 = f32[128,768]{1,0:T(8,128)} custom-call(f32[1024,256]{1,0:T(8,128)} %get-tuple-element.46.bc_ref, f32[1024,128]{1,0:T(8,128)} %get-tuple-element.48.cum_ref, bf16[1024,768]{1,0:T(8,128)(2,1)} %get-tuple-element.102.gy_ref), custom_call_target="tpu_custom_call" | custom-call | flops 1000000000 | bytes 3538944 | tf_op jit(solution)/shard_map/pallas_call | solution.py:618
  225.3 7.6 %convolution_convert_fusion.1 = bf16[1024,1536]{1,0:T(8,128)(2,1)} fusion(bf16[768,1536]{1,0:T(8,128)(2,1)} %get-tuple-element.53, f32[1024]{0:T(1024)S(1)} %bitcast.123, f32[768]{0:T(1024)S(1)} %copy-done.16, bf16[1024,768]{1,0:T(8,128)(2,1)} %convolution_convert_fusion.5, bf16[1024,768]{1,0:T(8,128)(2,1)} %get-tuple-element.50), kind=kOutput, calls=%fused_computation.14 | convolution fusion | flops 2425356288 | bytes 8657920 | tf_op jit(solution)/shard_map/dot_general | solution.py:732
  232.9 13.7 %collective-permute-done.1.ds_in_ref = f32[128,768]{1,0:T(8,128)S(1)} collective-permute-done((f32[128,768]{1,0:T(8,128)}, f32[128,768]{1,0:T(8,128)S(1)}, u32[]{:S(2)}, u32[]{:S(2)}) %collective-permute-start.1) | collective-permute-done | bytes 393248 | tf_op jit(solution)/shard_map/ppermute | solution.py:736
  247.3 33.6 %shard_map.232 = (f32[1024,768]{1,0:T(8,128)}, f32[1024,256]{1,0:T(8,128)}, f32[1024,128]{1,0:T(8,128)}, f32[8,768]{1,0:T(8,128)}, f32[8,256]{1,0:T(8,128)}, /*index=5*/f32[8,128]{1,0:T(8,128)}) custom-call(bf16[1040,768]{1,0:T(8,128)(2,1)} %convolution_convert_fusion.3.px_ref, bf16[1040,384]{1,0:T(8,128)(2,1)} %convolution_convert_fusion.4.pt_ref, ...), custom_call_target="tpu_custom_call" | custom-call | flops 1000000000 | bytes 19369984 | tf_op jit(solution)/shard_map/pallas_call | solution.py:618
  284.0 7.6 %fusion.70 = f32[1024,1536]{1,0:T(8,128)} fusion(bf16[1024,768]{1,0:T(8,128)(2,1)} %get-tuple-element.101, bf16[1536,768]{1,0:T(8,128)(2,1)} %bitcast.146), kind=kOutput, calls=%fused_computation.147 | convolution fusion | flops 2415919104 | bytes 10223616 | tf_op jit(solution)/shard_map/dot_general | solution.py:771
  293.6 7.4 %convolution_convert_fusion.2 = bf16[768,1536]{1,0:T(8,128)(2,1)} fusion(bf16[1024,1536]{1,0:T(8,128)(2,1)} %bitcast.143, f32[1024]{0:T(1024)S(1)} %bitcast.124, f32[768]{0:T(1024)} %copy-done.15, bf16[1024,768]{1,0:T(8,128)(2,1)} %convolution_convert_fusion.5, bf16[1024,768]{1,0:T(8,128)(2,1)} %get-tuple-element.50), kind=kOutput, calls=%fused_computation.20 | convolution fusion | flops 2424963072 | bytes 8657920 | tf_op jit(solution)/shard_map/tc,tf->cf/dot_general | solution.py:777
  306.5 6.3 %fusion.13 = bf16[1024,768]{1,0:T(8,128)(2,1)S(1)} fusion(f32[8,768]{1,0:T(8,128)S(1)} %slice.230, f32[1024,768]{1,0:T(8,128)} %get-tuple-element.56, f32[768]{0:T(1024)} %get-tuple-element.96, f32[768]{0:T(1024)} %get-tuple-element.97, f32[768]{0:T(1024)} %get-tuple-element.98, f32[768]{0:T(1024)} %get-tuple-element.95), kind=kLoop, calls=%fused_computation.31 | loop fusion | flops 8650752 | bytes 4755456 | tf_op jit(solution)/shard_map/convert_element_type | solution.py:751
  313.9 4.7 fusion.71
  319.6 6.5 %all_gather.3 = bf16[1024,256]{1,0:T(8,128)(2,1)S(1)} all-gather(bf16[256,256]{1,0:T(8,128)(2,1)S(1)} %convert_element_type.116), channel_id=1, replica_groups=mesh['dp'=4,'pair'=2,'quad'=4] {'quad'}, dimensions={0}, use_global_device_ids=true | all-gather | bytes 655360 | tf_op jit(solution)/shard_map/all_gather | solution.py:754
  327.6 10.6 %convolution_convert_fusion = bf16[1536,1664]{1,0:T(8,128)(2,1)} fusion(bf16[1024,1536]{1,0:T(8,128)(2,1)} %copy-done.4, bf16[1024,128]{1,0:T(8,128)(2,1)S(1)} %fusion.51, bf16[1024,768]{1,0:T(8,128)(2,1)} %copy-done.5, bf16[1024,768]{1,0:T(8,128)(2,1)} %get-tuple-element.101), kind=kOutput, calls=%fused_computation | convolution fusion | flops 5247270912 | bytes 11665408 | tf_op jit(solution)/shard_map/tc,tp->cp/dot_general | solution.py:776
  338.3 4.1 multiply_reduce_fusion
  342.4 2.9 concatenate.38
  345.9 183.6 %shard_map.233 = (bf16[4,384,1664]{2,1,0:T(8,128)(2,1)}, bf16[4,192,1536]{2,1,0:T(8,128)(2,1)}, f32[256,1536]{1,0:T(8,128)}, f32[256,1536]{1,0:T(8,128)}, f32[4,72,128]{2,1,0:T(8,128)}) custom-call(bf16[4,384,1664]{2,1,0:T(8,128)(2,1)} %bitcast.112, bf16[4,192,1536]{2,1,0:T(8,128)(2,1)} %bitcast.116, bf16[4,256,1536]{2,1,0:T(8,128)(2,1)} %bitcast.106, ...), custom_call_target="tpu_custom_call" | custom-call | flops 1000000 | bytes 24563712 | tf_op jit(solution)/shard_map/pallas_call | solution.py:596
  536.5 2.0 slice_bitcast_fusion.8
  540.3 4.3 slice_bitcast_fusion
  553.4 4.5 bitcast_convert_fusion
  557.9 8.8 %concatenate.39 = bf16[384,6448]{1,0:T(8,128)(2,1)} concatenate(bf16[384,768]{1,0:T(8,128)(2,1)} %get-tuple-element.121, bf16[384,768]{1,0:T(8,128)(2,1)} %get-tuple-element.120, bf16[384,768]{1,0:T(8,128)(2,1)} %get-tuple-element.119, bf16[384,768]{1,0:T(8,128)(2,1)} %get-tuple-element.118, bf16[384,768]{1,0:T(8,128)(2,1)} %get-tuple-element.117, ...), dimensions={1} | concatenate | bytes 9904128 | tf_op jit(solution)/shard_map/concatenate | solution.py:821
  566.8 7.8 %copy.36 = f32[384,6448]{0,1:T(8,128)} copy(bf16[384,6448]{1,0:T(8,128)(2,1)} %concatenate.39) | data formatting | bytes 14856192
  574.6 3.6 fusion.30
  (143 shorter events, 65.7 us)
Async XLA Ops:
  7.2 311.5 %reduce-scatter.2.cloned.1.call-start = ((), (), s32[]{:S(2)}) async-start(), calls=%async_computation.1 | async-start | bytes 1310720 | tf_op jit(solution)/shard_map/reduce_scatter | solution.py:753
  11.4 8.5 %copy-start.24 = (bf16[768]{0:T(1024)(128)(2,1)S(1)}, bf16[768]{0:T(1024)(128)(2,1)}, u32[]{:S(2)}) copy-start(bf16[768]{0:T(1024)(128)(2,1)} %param.23) | copy-start | bytes 4612
  11.4 8.6 %copy-start.25 = (bf16[384]{0:T(512)(128)(2,1)S(1)}, bf16[384]{0:T(512)(128)(2,1)}, u32[]{:S(2)}) copy-start(bf16[384]{0:T(512)(128)(2,1)} %param.14) | copy-start | bytes 2308
  123.6 5.1 copy-start
  128.7 2.5 copy-start.8
  129.5 1.7 copy-start.4
  142.2 17.7 %copy-start.14 = (f32[4,256]{1,0:T(4,128)S(1)}, f32[4,256]{1,0:T(4,128)}, u32[]{:S(2)}) copy-start(f32[4,256]{1,0:T(4,128)} %wb_ref.3) | copy-start | bytes 12292
  153.8 23.0 %collective-permute-start = (f32[128,768]{1,0:T(8,128)}, f32[128,768]{1,0:T(8,128)}, u32[]{:S(2)}, u32[]{:S(2)}) collective-permute-start(f32[128,768]{1,0:T(8,128)} %get-tuple-element.49), channel_id=1, source_target_pairs={{0,4},{1,5},{2,6},{3,7},{8,12},{9,13},{10,14},{11,15},{16,20},{17,... | collective-permute-start | bytes 1179656 | tf_op jit(solution)/shard_map/ppermute | solution.py:708
  166.7 26.5 %copy-start.15 = (f32[768]{0:T(1024)}, f32[768]{0:T(1024)S(1)}, u32[]{:S(2)}) copy-start(f32[768]{0:T(1024)S(1)} %dynamic_slice.42) | copy-start | bytes 9220
  166.7 1.7 copy-start.27
  217.6 7.7 %copy-start.16 = (f32[768]{0:T(1024)S(1)}, f32[768]{0:T(1024)}, u32[]{:S(2)}) copy-start(f32[768]{0:T(1024)} %copy-done.15) | copy-start | bytes 9220
  223.8 22.8 %collective-permute-start.1 = (f32[128,768]{1,0:T(8,128)}, f32[128,768]{1,0:T(8,128)S(1)}, u32[]{:S(2)}, u32[]{:S(2)}) collective-permute-start(f32[128,768]{1,0:T(8,128)} %shard_map.231), channel_id=1, source_target_pairs={{4,0},{5,1},{6,2},{7,3},{12,8},{13,9},{14,10},{15,11},{20,16},{21,... | collective-permute-start | bytes 1179656 | tf_op jit(solution)/shard_map/ppermute | solution.py:736
  282.4 9.2 %collective-permute-start.2 = (f32[8,1024]{1,0:T(8,128)S(1)}, f32[8,1024]{1,0:T(8,128)S(1)}, u32[]{:S(2)}, u32[]{:S(2)}) collective-permute-start(f32[8,1024]{1,0:T(8,128)S(1)} %pad_maximum_fusion.5), channel_id=1, source_target_pairs={{4,0},{5,1},{6,2},{7,3},{12,8},{13,9},{14,10},{15,11},{20,16},{21,... | collective-permute-start | bytes 98312 | tf_op jit(solution)/shard_map/ppermute | solution.py:745
  283.9 8.2 %copy-start.7 = (f32[1024,256]{1,0:T(8,128)S(1)}, f32[1024,256]{1,0:T(8,128)}, u32[]{:S(2)}) copy-start(f32[1024,256]{1,0:T(8,128)} %get-tuple-element.57) | copy-start | bytes 3145732
  283.9 8.2 %copy-start.20 = (f32[1,256]{1,0:T(1,128)S(1)}, f32[1,256]{1,0:T(1,128)}, u32[]{:S(2)}) copy-start(f32[1,256]{1,0:T(1,128)} %get-tuple-element.128) | copy-start | bytes 3076
  283.9 8.2 %copy-start.21 = (f32[1,256]{1,0:T(1,128)S(1)}, f32[1,256]{1,0:T(1,128)}, u32[]{:S(2)}) copy-start(f32[1,256]{1,0:T(1,128)} %get-tuple-element.129) | copy-start | bytes 3076
  284.0 8.2 %copy-start.22 = (f32[1,256]{1,0:T(1,128)S(1)}, f32[1,256]{1,0:T(1,128)}, u32[]{:S(2)}) copy-start(f32[1,256]{1,0:T(1,128)} %get-tuple-element.130) | copy-start | bytes 3076
  284.0 8.2 %copy-start.23 = (f32[1,256]{1,0:T(1,128)S(1)}, f32[1,256]{1,0:T(1,128)}, u32[]{:S(2)}) copy-start(f32[1,256]{1,0:T(1,128)} %get-tuple-element.131) | copy-start | bytes 3076
  293.6 7.4 %copy-start.11 = (f32[1024,128]{1,0:T(8,128)S(1)}, f32[1024,128]{1,0:T(8,128)}, u32[]{:S(2)}) copy-start(f32[1024,128]{1,0:T(8,128)} %get-tuple-element.58) | copy-start | bytes 1572868
  305.6 8.3 %copy-start.26 = (bf16[4,384,768]{2,1,0:T(8,128)(2,1)S(1)}, bf16[4,384,768]{2,1,0:T(8,128)(2,1)}, u32[]{:S(2)}) copy-start(bf16[4,384,768]{2,1,0:T(8,128)(2,1)} %get-tuple-element.43) | copy-start | bytes 7077892
  326.2 12.0 %slice-start = ((s8[6291456]{0:T(1024)(128)(4,1)}), s8[4194304]{0:T(1024)(128)(4,1)S(1)}, s32[]{:S(2)}) async-start(s8[6291456]{0:T(1024)(128)(4,1)} %bitcast.108), calls=%async_computation.2 | async-start | bytes 8388608
  326.3 11.9 %slice-start.2 = ((s8[6291456]{0:T(1024)(128)(4,1)}), s8[4194304]{0:T(1024)(128)(4,1)S(1)}, s32[]{:S(2)}) async-start(s8[6291456]{0:T(1024)(128)(4,1)} %bitcast.110), calls=%async_computation.4 | async-start | bytes 8388608
  327.6 10.7 %slice-start.1 = ((s8[6291456]{0:T(1024)(128)(4,1)}), s8[2097152]{0:T(1024)(128)(4,1)S(1)}, s32[]{:S(2)}) async-start(s8[6291456]{0:T(1024)(128)(4,1)} %bitcast.108), calls=%async_computation.3 | async-start | bytes 4194304
  327.6 10.6 %slice-start.3 = ((s8[6291456]{0:T(1024)(128)(4,1)}), s8[2097152]{0:T(1024)(128)(4,1)S(1)}, s32[]{:S(2)}) async-start(s8[6291456]{0:T(1024)(128)(4,1)} %bitcast.110), calls=%async_computation.5 | async-start | bytes 4194304
  327.6 10.6 %copy-start.6 = (bf16[1536,64]{1,0:T(8,128)(2,1)S(1)}, bf16[1536,64]{1,0:T(8,128)(2,1)}, u32[]{:S(2)}) copy-start(bf16[1536,64]{1,0:T(8,128)(2,1)} %constant_dynamic-slice_fusion.1) | copy-start | bytes 589828
  338.2 4.1 copy-start.13
  540.3 4.3 copy-start.1
  540.3 4.3 copy-start.2
  540.3 4.4 copy-start.17
  566.7 7.9 %copy-start.3 = (bf16[1,256,1536]{2,1,0:T(8,128)(2,1)S(1)}, bf16[1,256,1536]{2,1,0:T(8,128)(2,1)}, u32[]{:S(2)}) copy-start(bf16[1,256,1536]{2,1,0:T(8,128)(2,1)} %param.25) | copy-start | bytes 2359300
  566.7 7.9 %copy-start.18 = (f32[256]{0:T(256)S(1)}, f32[256]{0:T(256)}, u32[]{:S(2)}) copy-start(f32[256]{0:T(256)} %add_rsqrt_fusion.1) | copy-start | bytes 3076
  566.8 7.8 %copy-start.19 = (f32[256]{0:T(256)S(1)}, f32[256]{0:T(256)}, u32[]{:S(2)}) copy-start(f32[256]{0:T(256)} %broadcast_multiply_fusion) | copy-start | bytes 3076
  (4 other events, 3.3 us)
Sparse Core Ops, SparseCore 0:
  293.8 17.3 reduce-scatter.1
